TPU v7x, 32 devices: a 4x4x1 block of a 4x4x8 slice. The times are simulated.
32 devices in a mesh: dp: 1 (over z), tp: 4 (over y), pp: 8 (over x, core).
Axes of the slice: x: 4, y: 4, z: 1, core: 2. Of those that a mesh axis runs over, the one named last changes fastest.
The devices are a block of a 4x4x8 slice.
Arguments:
- x: bfloat16 [8, 256, 1024], P('dp')
- target: bfloat16 [8, 256, 1024], P('dp')
- w1: bfloat16 [8, 2, 1024, 4096], P(('dp', 'pp'), None, None, 'tp')
- w2: bfloat16 [8, 2, 4096, 1024], P(('dp', 'pp'), None, 'tp')
Outputs:
- output 1: float32 [8, 2, 1024, 4096], P(('dp', 'pp'), None, None, 'tp')
- output 2: float32 [8, 2, 4096, 1024], P(('dp', 'pp'), None, 'tp')
- output 3: float32 [1], P('dp')
All inputs are finite; a program needn't handle non-finite values.
Results may differ from a plain program's by a relative error of at most 0.0182704.
Values are sent between devices in bfloat16 or wider.
A program may use at most 768 MiB of HBM per device.

v0:
```python
import math
import jax
import jax.numpy as jnp
from jax import lax
from jax.sharding import PartitionSpec as P

GC = math.sqrt(2.0 / math.pi)


def gelu(v):
    return 0.5 * v * (1.0 + jnp.tanh(GC * (v + 0.044715 * v * v * v)))


def gelu_grad(v):
    t = jnp.tanh(GC * (v + 0.044715 * v * v * v))
    return 0.5 * (1.0 + t) + 0.5 * v * (1.0 - t * t) * GC * (1.0 + 0.134145 * v * v)


def layer_fwd(h, w1, w2):
    u = jnp.dot(h, w1, preferred_element_type=jnp.float32).astype(jnp.bfloat16)
    a = gelu(u.astype(jnp.float32)).astype(jnp.bfloat16)
    z = lax.psum(jnp.dot(a, w2, preferred_element_type=jnp.float32).astype(jnp.bfloat16), 'tp')
    return (h.astype(jnp.float32) + z.astype(jnp.float32)).astype(jnp.bfloat16), u


def layer_bwd(h, u, dh, w1, w2):
    uf = u.astype(jnp.float32)
    a = gelu(uf).astype(jnp.bfloat16)
    g = (gelu_grad(uf) * jnp.dot(dh, w2.T, preferred_element_type=jnp.float32)).astype(jnp.bfloat16)
    z = lax.psum(jnp.dot(g, w1.T, preferred_element_type=jnp.float32).astype(jnp.bfloat16), 'tp')
    dx = (dh.astype(jnp.float32) + z.astype(jnp.float32)).astype(jnp.bfloat16)
    return dx, jnp.dot(h.T, g, preferred_element_type=jnp.float32), jnp.dot(a.T, dh, preferred_element_type=jnp.float32)


def solution(mesh):
    npp = mesh.shape['pp']
    slots = 2 * npp - 1
    down = [(i, i + 1) for i in range(npp - 1)]
    up = [(i + 1, i) for i in range(npp - 1)]

    def body(x, target, w1, w2):
        nm, b, d = x.shape
        w1 = w1[0]
        w2 = w2[0]
        nl, _, fl = w1.shape
        s = lax.axis_index('pp')
        last = s == npp - 1
        scale = (nm * b) ** -0.5
        norm = 1.0 / (nm * b * d)
        saved_h = jnp.zeros((slots, nl, b, d), jnp.bfloat16)
        saved_u = jnp.zeros((slots, nl, b, fl), jnp.bfloat16)
        acc1 = [jnp.zeros((d, fl), jnp.float32) for _ in range(nl)]
        acc2 = [jnp.zeros((fl, d), jnp.float32) for _ in range(nl)]
        loss = jnp.zeros((), jnp.float32)
        recv_f = jnp.zeros((b, d), jnp.bfloat16)
        recv_b = jnp.zeros((b, d), jnp.bfloat16)
        for k in range(nm + 2 * npp - 2):
            has_f = k < nm + npp - 1
            has_b = k >= npp - 1
            if has_f:
                h = jnp.where(s == 0, x[min(k, nm - 1)], recv_f)
                for l in range(nl):
                    saved_h = saved_h.at[k % slots, l].set(h)
                    h, u = layer_fwd(h, w1[l], w2[l])
                    saved_u = saved_u.at[k % slots, l].set(u)
                out_f = h
            if has_b:
                mb = k - 2 * npp + 2 + s
                dh = recv_b
                if has_f:
                    diff = out_f.astype(jnp.float32) - target[k - npp + 1].astype(jnp.float32)
                    loss = loss + jnp.where(last, 0.5 * jnp.sum(diff * diff) * norm, 0.0)
                    dh = jnp.where(last, (diff * scale).astype(jnp.bfloat16), dh)
                dh = jnp.where((mb >= 0) & (mb < nm), dh, jnp.zeros_like(dh))
                slot = jnp.mod(mb + s, slots)
                hs = lax.dynamic_index_in_dim(saved_h, slot, 0, keepdims=False)
                us = lax.dynamic_index_in_dim(saved_u, slot, 0, keepdims=False)
                for l in reversed(range(nl)):
                    dh, d1, d2 = layer_bwd(hs[l], us[l], dh, w1[l], w2[l])
                    acc1[l] = acc1[l] + d1
                    acc2[l] = acc2[l] + d2
                recv_b = lax.ppermute(dh, 'pp', up)
            if has_f:
                recv_f = lax.ppermute(out_f, 'pp', down)
        loss = lax.psum(loss, 'pp')
        return jnp.stack(acc1)[None], jnp.stack(acc2)[None], loss.reshape(1)

    wspec1 = P(('dp', 'pp'), None, None, 'tp')
    wspec2 = P(('dp', 'pp'), None, 'tp', None)
    return jax.shard_map(body, mesh=mesh,
                         in_specs=(P('dp', None, None), P('dp', None, None), wspec1, wspec2),
                         out_specs=(wspec1, wspec2, P('dp')), check_vma=False)
```

profile of v0, /device:TPU:97, one launch (start us, length us, event | category | flops | bytes accessed | tf_op | source)
XLA Modules:
  0.0 2585.4 jit_solution(11812873737139710996)
XLA Ops:
  61.8 38.3 %all-reduce.64.cloned.1.call-done = bf16[256,1024]{1,0:T(8,128)(2,1)} async-done(((bf16[256,1024]{1,0:T(8,128)(2,1)}), bf16[256,1024]{1,0:T(8,128)(2,1)}) %all-reduce.64.cloned.1.call-update) | async-done | bytes 524304 | tf_op jit(solution)/shard_map/psum | solution.py:22
  120.6 37.0 %all-reduce.66.cloned.1.call-done = bf16[256,1024]{1,0:T(8,128)(2,1)} async-done(((bf16[256,1024]{1,0:T(8,128)(2,1)}), bf16[256,1024]{1,0:T(8,128)(2,1)}) %all-reduce.66.cloned.1.call-update) | async-done | bytes 524304 | tf_op jit(solution)/shard_map/psum | solution.py:22
  162.8 38.4 %all-reduce.68.cloned.1.call-done = bf16[256,1024]{1,0:T(8,128)(2,1)} async-done(((bf16[256,1024]{1,0:T(8,128)(2,1)}), bf16[256,1024]{1,0:T(8,128)(2,1)}) %all-reduce.68.cloned.1.call-update) | async-done | bytes 524304 | tf_op jit(solution)/shard_map/psum | solution.py:22
  220.2 37.0 %all-reduce.70.cloned.1.call-done = bf16[256,1024]{1,0:T(8,128)(2,1)} async-done(((bf16[256,1024]{1,0:T(8,128)(2,1)}), bf16[256,1024]{1,0:T(8,128)(2,1)}) %all-reduce.70.cloned.1.call-update) | async-done | bytes 524304 | tf_op jit(solution)/shard_map/psum | solution.py:22
  262.4 38.4 %all-reduce.72.cloned.1.call-done = bf16[256,1024]{1,0:T(8,128)(2,1)} async-done(((bf16[256,1024]{1,0:T(8,128)(2,1)}), bf16[256,1024]{1,0:T(8,128)(2,1)}) %all-reduce.72.cloned.1.call-update) | async-done | bytes 524304 | tf_op jit(solution)/shard_map/psum | solution.py:22
  319.9 37.0 %all-reduce.74.cloned.1.call-done = bf16[256,1024]{1,0:T(8,128)(2,1)} async-done(((bf16[256,1024]{1,0:T(8,128)(2,1)}), bf16[256,1024]{1,0:T(8,128)(2,1)}) %all-reduce.74.cloned.1.call-update) | async-done | bytes 524304 | tf_op jit(solution)/shard_map/psum | solution.py:22
  362.1 38.4 %all-reduce.76.cloned.1.call-done = bf16[256,1024]{1,0:T(8,128)(2,1)} async-done(((bf16[256,1024]{1,0:T(8,128)(2,1)}), bf16[256,1024]{1,0:T(8,128)(2,1)}) %all-reduce.76.cloned.1.call-update) | async-done | bytes 524304 | tf_op jit(solution)/shard_map/psum | solution.py:22
  419.6 37.0 %all-reduce.78.cloned.1.call-done = bf16[256,1024]{1,0:T(8,128)(2,1)} async-done(((bf16[256,1024]{1,0:T(8,128)(2,1)}), bf16[256,1024]{1,0:T(8,128)(2,1)}) %all-reduce.78.cloned.1.call-update) | async-done | bytes 524304 | tf_op jit(solution)/shard_map/psum | solution.py:22
  461.8 38.4 %all-reduce.80.cloned.1.call-done = bf16[256,1024]{1,0:T(8,128)(2,1)} async-done(((bf16[256,1024]{1,0:T(8,128)(2,1)}), bf16[256,1024]{1,0:T(8,128)(2,1)}) %all-reduce.80.cloned.1.call-update) | async-done | bytes 524304 | tf_op jit(solution)/shard_map/psum | solution.py:22
  519.3 37.0 %all-reduce.82.cloned.1.call-done = bf16[256,1024]{1,0:T(8,128)(2,1)} async-done(((bf16[256,1024]{1,0:T(8,128)(2,1)}), bf16[256,1024]{1,0:T(8,128)(2,1)}) %all-reduce.82.cloned.1.call-update) | async-done | bytes 524304 | tf_op jit(solution)/shard_map/psum | solution.py:22
  561.5 38.3 %all-reduce.84.cloned.1.call-done = bf16[256,1024]{1,0:T(8,128)(2,1)} async-done(((bf16[256,1024]{1,0:T(8,128)(2,1)}), bf16[256,1024]{1,0:T(8,128)(2,1)}) %all-reduce.84.cloned.1.call-update) | async-done | bytes 524304 | tf_op jit(solution)/shard_map/psum | solution.py:22
  661.0 38.3 %all-reduce.88.cloned.1.call-done = bf16[256,1024]{1,0:T(8,128)(2,1)} async-done(((bf16[256,1024]{1,0:T(8,128)(2,1)}), bf16[256,1024]{1,0:T(8,128)(2,1)}) %all-reduce.88.cloned.1.call-update) | async-done | bytes 524304 | tf_op jit(solution)/shard_map/psum | solution.py:22
  718.5 37.0 %all-reduce.90.cloned.1.call-done = bf16[256,1024]{1,0:T(8,128)(2,1)} async-done(((bf16[256,1024]{1,0:T(8,128)(2,1)}), bf16[256,1024]{1,0:T(8,128)(2,1)}) %all-reduce.90.cloned.1.call-update) | async-done | bytes 524304 | tf_op jit(solution)/shard_map/psum | solution.py:22
  819.1 39.5 %all-reduce.150.cloned.1.call-done = (bf16[256,1024]{1,0:T(8,128)(2,1)}, bf16[256,1024]{1,0:T(8,128)(2,1)}) async-done(((bf16[256,1024]{1,0:T(8,128)(2,1)}, bf16[256,1024]{1,0:T(8,128)(2,1)}), (bf16[256,1024]{1,0:T(8,128)(2,1)}, bf16[256,1024]{1,0:T(8,128)(2,1)})) %all-reduce.150.cloned.1.call-update) | async-done | bytes 1048592 | tf_op jit(solution)/shard_map/psum | solution.py:22
  866.8 42.0 %all-reduce.148.cloned.1.call-done = (bf16[256,1024]{1,0:T(8,128)(2,1)}, bf16[256,1024]{1,0:T(8,128)(2,1)}) async-done(((bf16[256,1024]{1,0:T(8,128)(2,1)}, bf16[256,1024]{1,0:T(8,128)(2,1)}), (bf16[256,1024]{1,0:T(8,128)(2,1)}, bf16[256,1024]{1,0:T(8,128)(2,1)})) %all-reduce.148.cloned.1.call-update) | async-done | bytes 1048592 | tf_op jit(solution)/shard_map/psum | solution.py:22
  959.7 40.6 %all-reduce.146.cloned.1.call-done = (bf16[256,1024]{1,0:T(8,128)(2,1)}, bf16[256,1024]{1,0:T(8,128)(2,1)}) async-done(((bf16[256,1024]{1,0:T(8,128)(2,1)}, bf16[256,1024]{1,0:T(8,128)(2,1)}), (bf16[256,1024]{1,0:T(8,128)(2,1)}, bf16[256,1024]{1,0:T(8,128)(2,1)})) %all-reduce.146.cloned.1.call-update) | async-done | bytes 1048592 | tf_op jit(solution)/shard_map/psum | solution.py:22
  1008.5 42.0 %all-reduce.144.cloned.1.call-done = (bf16[256,1024]{1,0:T(8,128)(2,1)}, bf16[256,1024]{1,0:T(8,128)(2,1)}) async-done(((bf16[256,1024]{1,0:T(8,128)(2,1)}, bf16[256,1024]{1,0:T(8,128)(2,1)}), (bf16[256,1024]{1,0:T(8,128)(2,1)}, bf16[256,1024]{1,0:T(8,128)(2,1)})) %all-reduce.144.cloned.1.call-update) | async-done | bytes 1048592 | tf_op jit(solution)/shard_map/psum | solution.py:22
  1101.7 40.6 %all-reduce.142.cloned.1.call-done = (bf16[256,1024]{1,0:T(8,128)(2,1)}, bf16[256,1024]{1,0:T(8,128)(2,1)}) async-done(((bf16[256,1024]{1,0:T(8,128)(2,1)}, bf16[256,1024]{1,0:T(8,128)(2,1)}), (bf16[256,1024]{1,0:T(8,128)(2,1)}, bf16[256,1024]{1,0:T(8,128)(2,1)})) %all-reduce.142.cloned.1.call-update) | async-done | bytes 1048592 | tf_op jit(solution)/shard_map/psum | solution.py:22
  1150.4 42.0 %all-reduce.140.cloned.1.call-done = (bf16[256,1024]{1,0:T(8,128)(2,1)}, bf16[256,1024]{1,0:T(8,128)(2,1)}) async-done(((bf16[256,1024]{1,0:T(8,128)(2,1)}, bf16[256,1024]{1,0:T(8,128)(2,1)}), (bf16[256,1024]{1,0:T(8,128)(2,1)}, bf16[256,1024]{1,0:T(8,128)(2,1)})) %all-reduce.140.cloned.1.call-update) | async-done | bytes 1048592 | tf_op jit(solution)/shard_map/psum | solution.py:22
  1243.5 40.6 %all-reduce.138.cloned.1.call-done = (bf16[256,1024]{1,0:T(8,128)(2,1)}, bf16[256,1024]{1,0:T(8,128)(2,1)}) async-done(((bf16[256,1024]{1,0:T(8,128)(2,1)}, bf16[256,1024]{1,0:T(8,128)(2,1)}), (bf16[256,1024]{1,0:T(8,128)(2,1)}, bf16[256,1024]{1,0:T(8,128)(2,1)})) %all-reduce.138.cloned.1.call-update) | async-done | bytes 1048592 | tf_op jit(solution)/shard_map/psum | solution.py:22
  1292.3 42.0 %all-reduce.136.cloned.1.call-done = (bf16[256,1024]{1,0:T(8,128)(2,1)}, bf16[256,1024]{1,0:T(8,128)(2,1)}) async-done(((bf16[256,1024]{1,0:T(8,128)(2,1)}, bf16[256,1024]{1,0:T(8,128)(2,1)}), (bf16[256,1024]{1,0:T(8,128)(2,1)}, bf16[256,1024]{1,0:T(8,128)(2,1)})) %all-reduce.136.cloned.1.call-update) | async-done | bytes 1048592 | tf_op jit(solution)/shard_map/psum | solution.py:22
  1385.7 40.2 %all-reduce.134.cloned.1.call-done = (bf16[256,1024]{1,0:T(8,128)(2,1)}, bf16[256,1024]{1,0:T(8,128)(2,1)}) async-done(((bf16[256,1024]{1,0:T(8,128)(2,1)}, bf16[256,1024]{1,0:T(8,128)(2,1)}), (bf16[256,1024]{1,0:T(8,128)(2,1)}, bf16[256,1024]{1,0:T(8,128)(2,1)})) %all-reduce.134.cloned.1.call-update) | async-done | bytes 1048592 | tf_op jit(solution)/shard_map/psum | solution.py:22
  1434.1 42.0 %all-reduce.132.cloned.1.call-done = (bf16[256,1024]{1,0:T(8,128)(2,1)}, bf16[256,1024]{1,0:T(8,128)(2,1)}) async-done(((bf16[256,1024]{1,0:T(8,128)(2,1)}, bf16[256,1024]{1,0:T(8,128)(2,1)}), (bf16[256,1024]{1,0:T(8,128)(2,1)}, bf16[256,1024]{1,0:T(8,128)(2,1)})) %all-reduce.132.cloned.1.call-update) | async-done | bytes 1048592 | tf_op jit(solution)/shard_map/psum | solution.py:22
  1528.1 40.4 %all-reduce.130.cloned.1.call-done = (bf16[256,1024]{1,0:T(8,128)(2,1)}, bf16[256,1024]{1,0:T(8,128)(2,1)}) async-done(((bf16[256,1024]{1,0:T(8,128)(2,1)}, bf16[256,1024]{1,0:T(8,128)(2,1)}), (bf16[256,1024]{1,0:T(8,128)(2,1)}, bf16[256,1024]{1,0:T(8,128)(2,1)})) %all-reduce.130.cloned.1.call-update) | async-done | bytes 1048592 | tf_op jit(solution)/shard_map/psum | solution.py:22
  (822 shorter events, 1620.6 us)
Async XLA Ops:
  61.8 95.8 %all-reduce.66.cloned.1.call-start = ((), (), s32[]{:S(2)}) async-start(), calls=%async_computation.2 | async-start | bytes 1048576 | tf_op jit(solution)/shard_map/psum | solution.py:22
  162.7 94.5 %all-reduce.70.cloned.1.call-start = ((), (), s32[]{:S(2)}) async-start(), calls=%async_computation.4 | async-start | bytes 1048576 | tf_op jit(solution)/shard_map/psum | solution.py:22
  262.4 94.6 %all-reduce.74.cloned.1.call-start = ((), (), s32[]{:S(2)}) async-start(), calls=%async_computation.6 | async-start | bytes 1048576 | tf_op jit(solution)/shard_map/psum | solution.py:22
  362.1 94.6 %all-reduce.78.cloned.1.call-start = ((), (), s32[]{:S(2)}) async-start(), calls=%async_computation.8 | async-start | bytes 1048576 | tf_op jit(solution)/shard_map/psum | solution.py:22
  461.8 94.5 %all-reduce.82.cloned.1.call-start = ((), (), s32[]{:S(2)}) async-start(), calls=%async_computation.10 | async-start | bytes 1048576 | tf_op jit(solution)/shard_map/psum | solution.py:22
  561.4 94.4 %all-reduce.86.cloned.1.call-start = ((), (), s32[]{:S(2)}) async-start(), calls=%async_computation.12 | async-start | bytes 1048576 | tf_op jit(solution)/shard_map/psum | solution.py:22
  661.0 94.5 %all-reduce.90.cloned.1.call-start = ((), (), s32[]{:S(2)}) async-start(), calls=%async_computation.14 | async-start | bytes 1048576 | tf_op jit(solution)/shard_map/psum | solution.py:22
  760.6 98.0 %all-reduce.150.cloned.1.call-start = ((), (), s32[]{:S(2)}) async-start(), calls=%async_computation.44 | async-start | bytes 2097152 | tf_op jit(solution)/shard_map/psum | solution.py:22
  866.7 133.7 %all-reduce.146.cloned.1.call-start = ((), (), s32[]{:S(2)}) async-start(), calls=%async_computation.42 | async-start | bytes 2097152 | tf_op jit(solution)/shard_map/psum | solution.py:22
  1008.5 133.8 %all-reduce.142.cloned.1.call-start = ((), (), s32[]{:S(2)}) async-start(), calls=%async_computation.40 | async-start | bytes 2097152 | tf_op jit(solution)/shard_map/psum | solution.py:22
  1150.4 133.7 %all-reduce.138.cloned.1.call-start = ((), (), s32[]{:S(2)}) async-start(), calls=%async_computation.38 | async-start | bytes 2097152 | tf_op jit(solution)/shard_map/psum | solution.py:22
  1243.4 90.9 %all-reduce.136.cloned.1.call-start = ((), (), s32[]{:S(2)}) async-start(), calls=%async_computation.37 | async-start | bytes 2097152 | tf_op jit(solution)/shard_map/psum | solution.py:22
  1292.2 133.6 %all-reduce.134.cloned.1.call-start = ((), (), s32[]{:S(2)}) async-start(), calls=%async_computation.36 | async-start | bytes 2097152 | tf_op jit(solution)/shard_map/psum | solution.py:22
  1434.1 134.4 %all-reduce.130.cloned.1.call-start = ((), (), s32[]{:S(2)}) async-start(), calls=%async_computation.34 | async-start | bytes 2097152 | tf_op jit(solution)/shard_map/psum | solution.py:22
  1576.5 138.5 %all-reduce.126.cloned.1.call-start = ((), (), s32[]{:S(2)}) async-start(), calls=%async_computation.32 | async-start | bytes 2097152 | tf_op jit(solution)/shard_map/psum | solution.py:22
  1674.3 92.6 %all-reduce.124.cloned.1.call-start = ((), (), s32[]{:S(2)}) async-start(), calls=%async_computation.31 | async-start | bytes 2097152 | tf_op jit(solution)/shard_map/psum | solution.py:30
  1724.9 99.6 %all-reduce.94.cloned.1.call-start = ((), (), s32[]{:S(2)}) async-start(), calls=%async_computation.16 | async-start | bytes 1048576 | tf_op jit(solution)/shard_map/psum | solution.py:30
  1829.3 93.0 %all-reduce.98.cloned.1.call-start = ((), (), s32[]{:S(2)}) async-start(), calls=%async_computation.18 | async-start | bytes 1048576 | tf_op jit(solution)/shard_map/psum | solution.py:30
  1928.3 93.1 %all-reduce.102.cloned.1.call-start = ((), (), s32[]{:S(2)}) async-start(), calls=%async_computation.20 | async-start | bytes 1048576 | tf_op jit(solution)/shard_map/psum | solution.py:30
  2028.2 93.7 %all-reduce.106.cloned.1.call-start = ((), (), s32[]{:S(2)}) async-start(), calls=%async_computation.22 | async-start | bytes 1048576 | tf_op jit(solution)/shard_map/psum | solution.py:30
  2128.6 92.4 %all-reduce.110.cloned.1.call-start = ((), (), s32[]{:S(2)}) async-start(), calls=%async_computation.24 | async-start | bytes 1048576 | tf_op jit(solution)/shard_map/psum | solution.py:30
  2227.1 92.6 %all-reduce.114.cloned.1.call-start = ((), (), s32[]{:S(2)}) async-start(), calls=%async_computation.26 | async-start | bytes 1048576 | tf_op jit(solution)/shard_map/psum | solution.py:30
  2325.7 92.3 %all-reduce.118.cloned.1.call-start = ((), (), s32[]{:S(2)}) async-start(), calls=%async_computation.28 | async-start | bytes 1048576 | tf_op jit(solution)/shard_map/psum | solution.py:30
  2424.1 99.2 %all-reduce.122.cloned.1.call-start = ((), (), s32[]{:S(2)}) async-start(), calls=%async_computation.30 | async-start | bytes 1048576 | tf_op jit(solution)/shard_map/psum | solution.py:30
  (244 other events, 4344.0 us)
Sparse Core Ops, SparseCore 0:
  12.1 39.6 all-reduce.61
  162.8 38.2 all-reduce.67
  262.5 38.3 all-reduce.71
  362.2 38.2 all-reduce.75
  760.7 38.3 all-reduce.91
  818.7 39.7 all-reduce.149
  866.8 41.9 all-reduce.147
  959.8 40.5 all-reduce.145
  1008.6 41.8 all-reduce.143
  1101.7 40.4 all-reduce.141
  1150.5 41.9 all-reduce.139
  1243.5 40.5 all-reduce.137
  1292.4 41.9 all-reduce.135
  1385.3 40.5 all-reduce.133
  1434.2 41.8 all-reduce.131
  1527.9 40.4 all-reduce.129
  1576.6 41.8 all-reduce.127
  1674.4 40.4 all-reduce.125
  1725.0 41.9 all-reduce.123
  1829.4 38.2 all-reduce.95
  1928.4 38.2 all-reduce.99
  2028.3 38.2 all-reduce.103
  2227.2 38.2 all-reduce.111
  2424.2 38.2 all-reduce.119
  (21 shorter events, 772.1 us)
where the time goes:
time: 2600 us; the launch traced here: 2590 us
  waiting for transfers between devices  1540 us (59%)
  matrix products  547 us (21%)
  local copies, waits for them, and re-layouts  216 us (8%)
  starting transfers between devices  140 us (5%)
  other arithmetic  111 us (4%)
    psum x29, waiting for transfers between devices, layer_fwd(): lax.psum(jnp.dot(a, w2, preferred_element_type=jnp.float32).astype(jnp.bf...  1070 us
    psum x16, waiting for transfers between devices, layer_bwd(): lax.psum(jnp.dot(g, w1.T, preferred_element_type=jnp.float32).astype(jnp....  417 us
    unnamed x404, local copies, waits for them, and re-layouts  204 us
    dot_general x30, matrix products, layer_bwd(): jnp.dot(a.T, dh, preferred_element_type=jnp.float32)  158 us
    dot_general x30, matrix products, layer_bwd(): jnp.dot(h.T, g, preferred_element_type=jnp.float32)  147 us
    dot_general x29, matrix products, layer_bwd(): jnp.dot(dh, w2.T, preferred_element_type=jnp.float32)  81.4 us
    ppermute x14, starting transfers between devices, body(): recv_b = lax.ppermute(dh, 'pp', up)  68.9 us
    ppermute x14, starting transfers between devices, body(): recv_f = lax.ppermute(out_f, 'pp', down)  67.2 us
  transfers between devices with their start and end apart: 73, of which 58 were waited for; matrix products, arithmetic and copies ran while one was open for 20% of the time, Pallas kernels for 0%

commit v1 on v0

v1 whole, which is shorter than its diff:
```python
import functools
import math
import jax
import jax.numpy as jnp
from jax import lax
from jax.experimental import pallas as pl
from jax.experimental.pallas import tpu as pltpu
from jax.sharding import PartitionSpec as P

GC = math.sqrt(2.0 / math.pi)
BF = jnp.bfloat16
F32 = jnp.float32
MESH = pl.DeviceIdType.MESH
CHUNK = 128


def gelu_parts(v):
    return jnp.tanh(GC * (v + 0.044715 * v * v * v))


def dot(a, b):
    return jnp.dot(a, b, preferred_element_type=F32)


def dot_t(a, b):
    return lax.dot_general(a, b, (((1,), (1,)), ((), ())), preferred_element_type=F32)


def dot_l(a, b):
    return lax.dot_general(a, b, (((0,), (0,)), ((), ())), preferred_element_type=F32)


def kernel(ntp, npp, scale, x_hbm, t_hbm, w1_hbm, w2_hbm, g1_hbm, g2_hbm, loss_ref,
           w1, w2, xs, ds, u, g, hs, hb, zs, zr, zsb, zrb, a_buf, zown, lacc, lbuf,
           in_sem, ws_sem, wr_sem, gs_sem, gr_sem, fl_s, fl_r, fa_s, fa_r, fz_s, fz_r,
           bl_s, bl_r, ba_s, ba_r, bz_s, bz_r, ls_sem, lr_sem):
    ntok, hd = hs.shape
    nl, d, fl = w1_hbm.shape
    ct = CHUNK
    nc = ntok // ct
    y = lax.axis_index('tp')
    pp = lax.axis_index('pp')
    c = lax.rem(pp, 2)
    o = 1 - c
    xc = lax.div(pp, 2)
    odd = lax.rem(xc, 2)
    r = y + odd * (ntp - 1 - 2 * y)
    k = xc * ntp + r
    nk = ntp * npp // 2
    first = k == 0
    last = k == nk - 1
    step = 1 - 2 * odd
    fwd_end = jnp.where(r == ntp - 1, 1, 0)
    bwd_end = jnp.where(r == 0, 1, 0)
    nxt = {'tp': y + step * (1 - fwd_end), 'pp': jnp.where(last, c, pp + 2 * fwd_end)}
    nxt['tp'] = jnp.where(last, 0, nxt['tp'])
    prv = {'tp': y - step * (1 - bwd_end), 'pp': jnp.where(first, npp - 2 + c, pp - 2 * bwd_end)}
    row_end = (ntp - 1) * (1 - lax.rem(npp // 2 - 1, 2))
    prv['tp'] = jnp.where(first, row_end, prv['tp'])
    mate = {'tp': y, 'pp': 2 * xc + o}

    barrier = pltpu.get_barrier_semaphore()
    for j in range(1, 2 * ntp):
        idx = lax.rem(y * 2 + c + j, 2 * ntp)
        pl.semaphore_signal(barrier, inc=1, device_id={'tp': lax.div(idx, 2), 'pp': 2 * xc + lax.rem(idx, 2)},
                            device_id_type=MESH)
    pl.semaphore_signal(barrier, inc=1, device_id=nxt, device_id_type=MESH)
    pl.semaphore_signal(barrier, inc=1, device_id=prv, device_id_type=MESH)
    pl.semaphore_wait(barrier, 2 * ntp + 1)

    def rcopy(src, dst, ss, rs, dev):
        return pltpu.make_async_remote_copy(src_ref=src, dst_ref=dst, send_sem=ss, recv_sem=rs,
                                            device_id=dev, device_id_type=MESH)

    for i in range(nl):
        rr = nl * c + i
        row = rr + odd * (ntp - 1 - 2 * rr)
        dst = {'tp': row, 'pp': 2 * xc + lax.div(y, 2)}
        same = (row == y) & (lax.div(y, 2) == c)
        b = lax.rem(y, 2)
        for n, (src, buf) in enumerate(((w1_hbm, w1), (w2_hbm, w2))):
            @pl.when(same)
            def _():
                pltpu.make_async_copy(src.at[i], buf.at[b], wr_sem.at[n, b]).start()

            @pl.when(jnp.logical_not(same))
            def _():
                rcopy(src.at[i], buf.at[b], ws_sem.at[n, i], wr_sem.at[n, b], dst).start()

    @pl.when(first)
    def _():
        for h in range(2):
            pltpu.make_async_copy(x_hbm.at[:, pl.ds(h * hd, hd)], xs.at[h], in_sem.at[h]).start()

    @pl.when(last)
    def _():
        pltpu.make_async_copy(t_hbm.at[:, pl.ds(pl.multiple_of(c * hd, hd), hd)], hs, in_sem.at[2]).start()

    lacc[...] = jnp.zeros_like(lacc)

    def wwait(n, b):
        src, buf = ((w1_hbm, w1), (w2_hbm, w2))[n]
        rcopy(src.at[0], buf.at[b], ws_sem.at[n, 0], wr_sem.at[n, b], mate).wait_recv()

    for n in range(2):
        for b in range(2):
            wwait(n, b)

    @pl.when(first)
    def _():
        for h in range(2):
            pltpu.make_async_copy(x_hbm.at[:, pl.ds(h * hd, hd)], xs.at[h], in_sem.at[h]).wait()

    @pl.when(last)
    def _():
        pltpu.make_async_copy(t_hbm.at[:, pl.ds(pl.multiple_of(c * hd, hd), hd)], hs, in_sem.at[2]).wait()

    def rows(m):
        return pl.ds(pl.multiple_of(m * ct, ct), ct)

    def cp_link(buf, store, m, ss, rs, dev):
        return rcopy(buf.at[rows(m)], store.at[c, rows(m)], ss.at[m], rs.at[m], dev)

    def cp_ag(store, half, m, ss, rs):
        return rcopy(store.at[half, rows(m)], store.at[half, rows(m)], ss.at[m], rs.at[m], mate)

    def cp_rs(src, dst, m, ss, rs):
        return rcopy(src.at[rows(m)], dst.at[rows(m)], ss.at[m], rs.at[m], mate)

    def get_f(m):
        cp_link(hs, xs, m, fl_s, fl_r, nxt).wait_recv()
        cp_ag(xs, c, m, fa_s, fa_r).start()

    @pl.when(jnp.logical_not(first))
    def _():
        get_f(0)

    half_o = pl.ds(pl.multiple_of(o * hd, hd), hd)
    half_c = pl.ds(pl.multiple_of(c * hd, hd), hd)
    tn = fl // 2

    def fwd(m, _):
        @pl.when(jnp.logical_not(first))
        def _():
            cp_ag(xs, o, m, fa_s, fa_r).wait_recv()

        rw = rows(m)
        for q in range(2):
            for t in range(fl // tn):
                s = pl.ds(t * tn, tn)
                v = (dot(xs[0, rw, :], w1[q, :hd, s]) + dot(xs[1, rw, :], w1[q, hd:, s])).astype(BF)
                u[q, rw, s] = v
                v = v.astype(F32)
                a_buf[q, :, s] = (0.5 * v * (1.0 + gelu_parts(v))).astype(BF)
        zs[rw, :] = (dot(a_buf[0], w2[0, :, half_o]) + dot(a_buf[1], w2[1, :, half_o])).astype(BF)
        cp_rs(zs, zr, m, fz_s, fz_r).start()
        zown[...] = (xs[c, rw, :].astype(F32)
                     + (dot(a_buf[0], w2[0, :, half_c]) + dot(a_buf[1], w2[1, :, half_c])))

        @pl.when(jnp.logical_not(first) & (m + 1 < nc))
        def _():
            get_f(m + 1)

        cp_rs(zs, zr, m, fz_s, fz_r).wait_recv()
        out = (zown[...] + zr[rw, :].astype(F32)).astype(BF)

        @pl.when(jnp.logical_not(last))
        def _():
            hs[rw, :] = out
            cp_link(hs, xs, m, fl_s, fl_r, nxt).start()

        @pl.when(last)
        def _():
            diff = out.astype(F32) - hs[rw, :].astype(F32)
            ds[c, rw, :] = (diff * scale).astype(BF)
            sq = jnp.sum((diff * diff).reshape(ct // 8, 8, hd), axis=0)
            tot = lacc[...]
            for j in range(hd // 128):
                tot = tot + sq[:, j * 128:(j + 1) * 128]
            lacc[...] = tot

        return 0

    lax.fori_loop(0, nc, fwd, 0)

    def get_b(m):
        @pl.when(jnp.logical_not(last))
        def _():
            cp_link(hb, ds, m, bl_s, bl_r, prv).wait_recv()

        cp_ag(ds, c, m, ba_s, ba_r).start()

    get_b(0)

    def bwd(m, _):
        cp_ag(ds, o, m, ba_s, ba_r).wait_recv()
        rw = rows(m)
        for q in range(2):
            for t in range(fl // tn):
                s = pl.ds(t * tn, tn)
                da = dot_t(ds[0, rw, :], w2[q, s, :hd]) + dot_t(ds[1, rw, :], w2[q, s, hd:])
                v = u[q, rw, s].astype(F32)
                th = gelu_parts(v)
                gp = 0.5 * (1.0 + th) + 0.5 * v * (1.0 - th * th) * GC * (1.0 + 0.134145 * v * v)
                g[q, rw, s] = (gp * da).astype(BF)
                u[q, rw, s] = (0.5 * v * (1.0 + th)).astype(BF)

        @pl.when(jnp.logical_not(first))
        def _():
            zsb[rw, :] = (dot_t(g[0, rw, :], w1[0, half_o, :]) + dot_t(g[1, rw, :], w1[1, half_o, :])).astype(BF)
            cp_rs(zsb, zrb, m, bz_s, bz_r).start()
            zown[...] = (ds[c, rw, :].astype(F32)
                         + (dot_t(g[0, rw, :], w1[0, half_c, :]) + dot_t(g[1, rw, :], w1[1, half_c, :])))

        @pl.when(m + 1 < nc)
        def _():
            get_b(m + 1)

        @pl.when(jnp.logical_not(first))
        def _():
            cp_rs(zsb, zrb, m, bz_s, bz_r).wait_recv()
            hb[rw, :] = (zown[...] + zrb[rw, :].astype(F32)).astype(BF)
            cp_link(hb, ds, m, bl_s, bl_r, prv).start()

        return 0

    lax.fori_loop(0, nc, bwd, 0)

    @pl.when(last)
    def _():
        lbuf[0] = lacc[...]
        cp = rcopy(lbuf.at[0], lbuf.at[1], ls_sem.at[0], lr_sem.at[0], mate)
        cp.start()
        cp.wait()
        lbuf[2] = lbuf[0] + lbuf[1]

    @pl.when(jnp.logical_not(last))
    def _():
        rcopy(lbuf.at[2], lbuf.at[2], ls_sem.at[1], lr_sem.at[1], prv).wait_recv()

    @pl.when(jnp.logical_not(first))
    def _():
        rcopy(lbuf.at[2], lbuf.at[2], ls_sem.at[1], lr_sem.at[1], prv).start()

    i_own = lax.rem(r, nl)
    src_core = lax.div(r, nl)

    def send_g(n, b, wait):
        buf, out = ((w1, g1_hbm), (w2, g2_hbm))[n]
        row = 2 * c + b
        same = (row == y) & (src_core == c)
        dst = {'tp': row, 'pp': 2 * xc + src_core}

        if not wait:
            @pl.when(same)
            def _():
                pltpu.make_async_copy(buf.at[b], out.at[i_own], gr_sem.at[n, i_own]).start()

        @pl.when(jnp.logical_not(same))
        def _():
            cp = rcopy(buf.at[b], out.at[i_own], gs_sem.at[n, b], gr_sem.at[n, i_own], dst)
            if wait:
                cp.wait_send()
            else:
                cp.start()

    tm = 256

    for b in range(2):
        def dw2(t, _):
            s = pl.ds(pl.multiple_of(t * tm, tm), tm)
            for h in range(2):
                w2[b, s, h * hd:(h + 1) * hd] = dot_l(u[b, :, s], ds[h]).astype(BF)
            return 0

        lax.fori_loop(0, fl // tm, dw2, 0)
        send_g(1, b, False)
    for b in range(2):
        for h in range(2):
            def dw1(t, _):
                s = pl.ds(pl.multiple_of(t * tm, tm), tm)
                w1[b, pl.ds(pl.multiple_of(h * hd + t * tm, tm), tm), :] = dot_l(xs[h, :, s], g[b]).astype(BF)
                return 0

            lax.fori_loop(0, hd // tm, dw1, 0)
        send_g(0, b, False)

    loss_ref[...] = lbuf[2]

    for i in range(nl):
        rr = nl * c + i
        row = rr + odd * (ntp - 1 - 2 * rr)
        same = (row == y) & (lax.div(y, 2) == c)
        for n, (src, buf) in enumerate(((w1_hbm, w1), (w2_hbm, w2))):
            @pl.when(jnp.logical_not(same))
            def _():
                rcopy(src.at[i], buf.at[0], ws_sem.at[n, i], wr_sem.at[n, 0], mate).wait_send()

    def drain(m, _):
        cp_rs(zs, zr, m, fz_s, fz_r).wait_send()
        cp_ag(ds, c, m, ba_s, ba_r).wait_send()

        @pl.when(jnp.logical_not(last))
        def _():
            cp_link(hs, xs, m, fl_s, fl_r, nxt).wait_send()

        @pl.when(jnp.logical_not(first))
        def _():
            cp_ag(xs, c, m, fa_s, fa_r).wait_send()
            cp_rs(zsb, zrb, m, bz_s, bz_r).wait_send()
            cp_link(hb, ds, m, bl_s, bl_r, prv).wait_send()

        return 0

    lax.fori_loop(0, nc, drain, 0)

    @pl.when(jnp.logical_not(first))
    def _():
        rcopy(lbuf.at[2], lbuf.at[2], ls_sem.at[1], lr_sem.at[1], prv).wait_send()

    for n in range(2):
        buf, out = ((w1, g1_hbm), (w2, g2_hbm))[n]
        for b in range(2):
            send_g(n, b, True)
        for i in range(nl):
            rcopy(buf.at[0], out.at[i], gs_sem.at[n, 0], gr_sem.at[n, i], mate).wait_recv()


def solution(mesh):
    ntp = mesh.shape['tp']
    npp = mesh.shape['pp']

    def body(x, target, w1, w2):
        nm, b, d = x.shape
        _, nl, _, fl = w1.shape
        ntok = nm * b
        hd = d // 2
        nc = ntok // CHUNK
        dma = pltpu.SemaphoreType.DMA
        any_ = pl.BlockSpec(memory_space=pl.ANY)
        vm = pltpu.VMEM
        g1, g2, loss = pl.pallas_call(
            functools.partial(kernel, ntp, npp, (nm * b) ** -0.5),
            out_shape=(jax.ShapeDtypeStruct((nl, d, fl), BF), jax.ShapeDtypeStruct((nl, fl, d), BF),
                       jax.ShapeDtypeStruct((8, 128), F32)),
            in_specs=[any_] * 4,
            out_specs=(any_, any_, pl.BlockSpec(memory_space=pltpu.VMEM)),
            scratch_shapes=[
                vm((2, d, fl), BF), vm((2, fl, d), BF),
                vm((2, ntok, hd), BF), vm((2, ntok, hd), BF),
                vm((2, ntok, fl), BF), vm((2, ntok, fl), BF),
                vm((ntok, hd), BF), vm((ntok, hd), BF),
                vm((ntok, hd), BF), vm((ntok, hd), BF), vm((ntok, hd), BF), vm((ntok, hd), BF),
                vm((2, CHUNK, fl), BF), vm((CHUNK, hd), F32), vm((8, 128), F32), vm((3, 8, 128), F32),
                dma((3,)), dma((2, nl)), dma((2, 2)), dma((2, 2)), dma((2, nl)),
                dma((nc,)), dma((nc,)), dma((nc,)), dma((nc,)), dma((nc,)), dma((nc,)),
                dma((nc,)), dma((nc,)), dma((nc,)), dma((nc,)), dma((nc,)), dma((nc,)),
                dma((2,)), dma((2,)),
            ],
            compiler_params=pltpu.CompilerParams(collective_id=0, has_side_effects=True,
                                                 vmem_limit_bytes=62 * 2 ** 20),
            name='step',
        )(x.reshape(ntok, d), target.reshape(ntok, d), w1[0], w2[0])
        loss = jnp.sum(loss) * (0.5 / (nm * b * d))
        return g1.astype(F32)[None], g2.astype(F32)[None], loss.reshape(1)

    wspec1 = P(('dp', 'pp'), None, None, 'tp')
    wspec2 = P(('dp', 'pp'), None, 'tp', None)
    return jax.shard_map(body, mesh=mesh,
                         in_specs=(P('dp', None, None), P('dp', None, None), wspec1, wspec2),
                         out_specs=(wspec1, wspec2, P('dp')), check_vma=False)
```

time: 2600 us -> 621 us (0.24)
  waiting for transfers between devices: 1540 us -> 0 us
  Pallas kernels: 0 us -> 606 us
  matrix products: 547 us -> 0 us
  local copies, waits for them, and re-layouts: 216 us -> 0 us
  starting transfers between devices: 140 us -> 0 us
  other arithmetic: 111 us -> 13.1 us
    psum x45 -> x0, waiting for transfers between devices: 1480 us -> none  [the longest x29 1070 us: layer_fwd(): lax.psum(jnp.dot(a, w2, preferred_element_type=jnp.float32).astype(jnp.bf...]
    pallas_call x0 -> x1, Pallas kernels: none -> 606 us  [body(): pl.pallas_call(functools.partial(kernel, ntp, npp, (nm * b) ** (-0.5)), o...]
    dot_general x178 -> x0, matrix products: 547 us -> none  [the longest x30 158 us: layer_bwd(): jnp.dot(a.T, dh, preferred_element_type=jnp.float32)]
    unnamed x404 -> x0, local copies, waits for them, and re-layouts: 204 us -> none
    ppermute x28 -> x0, starting transfers between devices: 136 us -> none  [the longest x14 68.9 us: body(): recv_b = lax.ppermute(dh, 'pp', up)]
    ppermute x28 -> x0, waiting for transfers between devices: 48.6 us -> none  [the longest x14 48.6 us: body(): recv_f = lax.ppermute(out_f, 'pp', down)]
    scatter x29 -> x0, other arithmetic: 46.8 us -> none  [body(): saved_h = saved_h.at[k % slots, l].set(h)]
    convert_element_type x27 -> x0, other arithmetic: 36.5 us -> none  [the longest x20 26.4 us: layer_bwd(): dx = (dh.astype(jnp.float32) + z.astype(jnp.float32)).astype(jnp.bfloat16)]
  transfers between devices with their start and end apart: 73 -> 0, of which waited for: 58 -> 0; matrix products, arithmetic and copies ran while one was open for 20% -> 0% of each run, Pallas kernels for 0% -> 0%
where the time goes in v1:
time: 621 us
  Pallas kernels  606 us (98%)
  other arithmetic  13.1 us (2%)
    pallas_call x1, Pallas kernels, body(): pl.pallas_call(functools.partial(kernel, ntp, npp, (nm * b) ** (-0.5)), o...  606 us

profile of v1, /device:TPU:97, one launch (start us, length us, event | category | flops | bytes accessed | tf_op | source)
XLA Modules:
  0.0 621.3 jit_solution(7707354790389991263)
XLA Ops:
  0.6 605.8 %step.1 = (bf16[2,1024,1024]{2,1,0:T(8,128)(2,1)}, bf16[2,1024,1024]{2,1,0:T(8,128)(2,1)}, f32[8,128]{1,0:T(8,128)}) custom-call(bf16[2048,1024]{1,0:T(8,128)(2,1)} %bitcast.11, bf16[2048,1024]{1,0:T(8,128)(2,1)} %bitcast.12, bf16[2,1024,1024]{2,1,0:T(8,128)(2,1)} %bitcast.13, bf16[2,1024,1024]{2,1,0:T(8,128)(2,1)} %bitcast.14), custom_call_target="tpu_custom_call" | custom-call | tf_op jit(solution)/shard_map/step/pallas_call | solution.py:342
  606.5 1.3 reduce_sum.9
  608.4 11.8 %bitcast_convert_fusion = (f32[1,2,1024,1024]{3,2,1,0:T(8,128)}, f32[1,2,1024,1024]{3,2,1,0:T(8,128)}) fusion(bf16[2,1024,1024]{2,1,0:T(8,128)(2,1)} %get-tuple-element.7, bf16[2,1024,1024]{2,1,0:T(8,128)(2,1)} %get-tuple-element.6), kind=kLoop, calls=%fused_computation | loop fusion | flops 4194304 | bytes 25165824 | tf_op jit(solution)/shard_map/broadcast_in_dim | solution.py:365

commit v2 on v1

--- a/solution.py
+++ b/solution.py
@@ -12,6 +12,8 @@
 F32 = jnp.float32
 MESH = pl.DeviceIdType.MESH
 CHUNK = 128
+PARTS = 4
+VIA = 3
 
 
 def gelu_parts(v):
@@ -22,17 +24,13 @@
     return jnp.dot(a, b, preferred_element_type=F32)
 
 
-def dot_t(a, b):
-    return lax.dot_general(a, b, (((1,), (1,)), ((), ())), preferred_element_type=F32)
-
-
 def dot_l(a, b):
     return lax.dot_general(a, b, (((0,), (0,)), ((), ())), preferred_element_type=F32)
 
 
 def kernel(ntp, npp, scale, x_hbm, t_hbm, w1_hbm, w2_hbm, g1_hbm, g2_hbm, loss_ref,
-           w1, w2, xs, ds, u, g, hs, hb, zs, zr, zsb, zrb, a_buf, zown, lacc, lbuf,
-           in_sem, ws_sem, wr_sem, gs_sem, gr_sem, fl_s, fl_r, fa_s, fa_r, fz_s, fz_r,
+           w1, w2, w1t, w2t, xs, ds, u, g, hs, hb, zs, zr, zsb, zrb, a_buf, zown, lacc, lbuf, rw1, rw2, rg1, rg2,
+           in_sem, ws_sem, wr_sem, gs_sem, gr_sem, rws, rwr, rgs, rgr, fl_s, fl_r, fa_s, fa_r, fz_s, fz_r,
            bl_s, bl_r, ba_s, ba_r, bz_s, bz_r, ls_sem, lr_sem):
     ntok, hd = hs.shape
     nl, d, fl = w1_hbm.shape
@@ -66,26 +64,90 @@
                             device_id_type=MESH)
     pl.semaphore_signal(barrier, inc=1, device_id=nxt, device_id_type=MESH)
     pl.semaphore_signal(barrier, inc=1, device_id=prv, device_id_type=MESH)
-    pl.semaphore_wait(barrier, 2 * ntp + 1)
+    ncol = npp // 2
+    src_col = xc == 0
+    rel_col = xc == ncol - 1
+    edge = src_col | rel_col
+    other_col = ncol - 1 - xc
+
+    @pl.when(edge)
+    def _():
+        for j in range(2 * ntp):
+            pl.semaphore_signal(barrier, inc=1, device_id={'tp': j // 2, 'pp': 2 * other_col + j % 2},
+                                device_id_type=MESH)
+
+    pl.semaphore_wait(barrier, 2 * ntp + 1 + jnp.where(edge, 2 * ntp, 0))
 
     def rcopy(src, dst, ss, rs, dev):
         return pltpu.make_async_remote_copy(src_ref=src, dst_ref=dst, send_sem=ss, recv_sem=rs,
                                             device_id=dev, device_id_type=MESH)
 
-    for i in range(nl):
+    rp = d // PARTS
+    parts = [pl.ds(p * rp, rp) for p in range(PARTS)]
+    wsrc = (w1_hbm, w2_hbm)
+    wbuf = (w1, w2)
+    rwb = (rw1, rw2)
+    rgb = (rg1, rg2)
+    gout = (g1_hbm, g2_hbm)
+    cq = lax.div(y, 2)
+    bq = lax.rem(y, 2)
+    far = lax.rem(y + ntp // 2, ntp)
+    kd = PARTS - VIA
+
+    def w_copy(i, n, p):
         rr = nl * c + i
         row = rr + odd * (ntp - 1 - 2 * rr)
-        dst = {'tp': row, 'pp': 2 * xc + lax.div(y, 2)}
-        same = (row == y) & (lax.div(y, 2) == c)
-        b = lax.rem(y, 2)
-        for n, (src, buf) in enumerate(((w1_hbm, w1), (w2_hbm, w2))):
-            @pl.when(same)
-            def _():
-                pltpu.make_async_copy(src.at[i], buf.at[b], wr_sem.at[n, b]).start()
-
+        src, dst = wsrc[n].at[i, parts[p]], wbuf[n].at[bq, parts[p]]
+        ss, rs = ws_sem.at[n, i, p], wr_sem.at[n, bq, p]
+        same = (row == y) & (cq == c)
+        direct = functools.partial(rcopy, src, dst, ss, rs, {'tp': row, 'pp': 2 * xc + cq})
+        relay = functools.partial(rcopy, src, rwb[n].at[max(p - kd, 0)], ss, rwr.at[n, max(p - kd, 0)],
+                                  {'tp': row, 'pp': 2 * (ncol - 1) + cq})
+        local = functools.partial(pltpu.make_async_copy, src, dst, rs)
+        return same, src_col & (row == far), direct, relay, local
+
+    def send(same, via, direct, relay, local, p):
+        @pl.when(same)
+        def _():
+            local().start()
+
+        if p < kd:
             @pl.when(jnp.logical_not(same))
             def _():
-                rcopy(src.at[i], buf.at[b], ws_sem.at[n, i], wr_sem.at[n, b], dst).start()
+                direct().start()
+        else:
+            @pl.when(jnp.logical_not(same) & jnp.logical_not(via))
+            def _():
+                direct().start()
+
+            @pl.when(via)
+            def _():
+                relay().start()
+
+    def send_w():
+        for n in range(2):
+            for p in reversed(range(PARTS)):
+                for i in range(nl):
+                    send(*w_copy(i, n, p), p)
+
+    home = {'tp': y, 'pp': c}
+    far_b = lax.rem(far, 2)
+    far_i = lax.rem(far, nl)
+
+    def relay_w():
+        for wait in (False, True):
+            for n in range(2):
+                for p in reversed(range(kd, PARTS)):
+                    slot = rwb[n].at[p - kd]
+                    fwd_cp = rcopy(slot, wbuf[n].at[far_b, parts[p]], rws.at[n, p - kd], wr_sem.at[n, far_b, p], home)
+                    if wait:
+                        fwd_cp.wait_send()
+                    else:
+                        rcopy(slot, slot, rws.at[n, p - kd], rwr.at[n, p - kd], home).wait_recv()
+                        fwd_cp.start()
+
+    pl.when(rel_col & (lax.div(far, 2) == c))(relay_w)
+    send_w()
 
     @pl.when(first)
     def _():
@@ -98,13 +160,11 @@
 
     lacc[...] = jnp.zeros_like(lacc)
 
-    def wwait(n, b):
-        src, buf = ((w1_hbm, w1), (w2_hbm, w2))[n]
-        rcopy(src.at[0], buf.at[b], ws_sem.at[n, 0], wr_sem.at[n, b], mate).wait_recv()
-
     for n in range(2):
         for b in range(2):
-            wwait(n, b)
+            for p in range(PARTS):
+                rcopy(wsrc[n].at[0, parts[p]], wbuf[n].at[b, parts[p]], ws_sem.at[n, 0, p], wr_sem.at[n, b, p],
+                      mate).wait_recv()
 
     @pl.when(first)
     def _():
@@ -181,7 +241,26 @@
 
         return 0
 
+    def transpose_w():
+        tt = 256
+        for b in range(2):
+            def t1(t, _):
+                s = pl.ds(pl.multiple_of(t * tt, tt), tt)
+                w1t[b, :, s] = w1[b, s, :].T
+                return 0
+
+            def t2(t, _):
+                s = pl.ds(pl.multiple_of(t * tt, tt), tt)
+                w2t[b, :, s] = w2[b, s, :].T
+                return 0
+
+            lax.fori_loop(0, d // tt, t1, 0)
+            lax.fori_loop(0, fl // tt, t2, 0)
+
+    early = k >= nk // 2
+    pl.when(early)(transpose_w)
     lax.fori_loop(0, nc, fwd, 0)
+    pl.when(jnp.logical_not(early))(transpose_w)
 
     def get_b(m):
         @pl.when(jnp.logical_not(last))
@@ -198,7 +277,7 @@
         for q in range(2):
             for t in range(fl // tn):
                 s = pl.ds(t * tn, tn)
-                da = dot_t(ds[0, rw, :], w2[q, s, :hd]) + dot_t(ds[1, rw, :], w2[q, s, hd:])
+                da = dot(ds[0, rw, :], w2t[q, :hd, s]) + dot(ds[1, rw, :], w2t[q, hd:, s])
                 v = u[q, rw, s].astype(F32)
                 th = gelu_parts(v)
                 gp = 0.5 * (1.0 + th) + 0.5 * v * (1.0 - th * th) * GC * (1.0 + 0.134145 * v * v)
@@ -207,10 +286,10 @@
 
         @pl.when(jnp.logical_not(first))
         def _():
-            zsb[rw, :] = (dot_t(g[0, rw, :], w1[0, half_o, :]) + dot_t(g[1, rw, :], w1[1, half_o, :])).astype(BF)
+            zsb[rw, :] = (dot(g[0, rw, :], w1t[0, :, half_o]) + dot(g[1, rw, :], w1t[1, :, half_o])).astype(BF)
             cp_rs(zsb, zrb, m, bz_s, bz_r).start()
             zown[...] = (ds[c, rw, :].astype(F32)
-                         + (dot_t(g[0, rw, :], w1[0, half_c, :]) + dot_t(g[1, rw, :], w1[1, half_c, :])))
+                         + (dot(g[0, rw, :], w1t[0, :, half_c]) + dot(g[1, rw, :], w1t[1, :, half_c])))
 
         @pl.when(m + 1 < nc)
         def _():
@@ -245,24 +324,32 @@
     i_own = lax.rem(r, nl)
     src_core = lax.div(r, nl)
 
-    def send_g(n, b, wait):
-        buf, out = ((w1, g1_hbm), (w2, g2_hbm))[n]
+    def g_copy(n, b, p):
         row = 2 * c + b
+        src, dst = wbuf[n].at[b, parts[p]], gout[n].at[i_own, parts[p]]
+        ss, rs = gs_sem.at[n, b, p], gr_sem.at[n, i_own, p]
         same = (row == y) & (src_core == c)
-        dst = {'tp': row, 'pp': 2 * xc + src_core}
-
-        if not wait:
-            @pl.when(same)
-            def _():
-                pltpu.make_async_copy(buf.at[b], out.at[i_own], gr_sem.at[n, i_own]).start()
-
-        @pl.when(jnp.logical_not(same))
-        def _():
-            cp = rcopy(buf.at[b], out.at[i_own], gs_sem.at[n, b], gr_sem.at[n, i_own], dst)
-            if wait:
-                cp.wait_send()
-            else:
-                cp.start()
+        direct = functools.partial(rcopy, src, dst, ss, rs, {'tp': row, 'pp': 2 * xc + src_core})
+        relay = functools.partial(rcopy, src, rgb[n].at[max(p - kd, 0)], ss, rgr.at[n, max(p - kd, 0)],
+                                  {'tp': row, 'pp': 2 * (ncol - 1) + src_core})
+        local = functools.partial(pltpu.make_async_copy, src, dst, rs)
+        return same, src_col & (row == far), direct, relay, local
+
+    def send_g(n, b):
+        for p in reversed(range(PARTS)):
+            send(*g_copy(n, b, p), p)
+
+    def relay_g():
+        for wait in (False, True):
+            for n in (1, 0):
+                for p in reversed(range(kd, PARTS)):
+                    slot = rgb[n].at[p - kd]
+                    fwd_cp = rcopy(slot, gout[n].at[far_i, parts[p]], rgs.at[n, p - kd], gr_sem.at[n, far_i, p], home)
+                    if wait:
+                        fwd_cp.wait_send()
+                    else:
+                        rcopy(slot, slot, rgs.at[n, p - kd], rgr.at[n, p - kd], home).wait_recv()
+                        fwd_cp.start()
 
     tm = 256
 
@@ -274,7 +361,7 @@
             return 0
 
         lax.fori_loop(0, fl // tm, dw2, 0)
-        send_g(1, b, False)
+        send_g(1, b)
     for b in range(2):
         for h in range(2):
             def dw1(t, _):
@@ -283,18 +370,19 @@
                 return 0
 
             lax.fori_loop(0, hd // tm, dw1, 0)
-        send_g(0, b, False)
+        send_g(0, b)
 
     loss_ref[...] = lbuf[2]
+    pl.when(rel_col & (lax.div(far, nl) == c))(relay_g)
 
     for i in range(nl):
-        rr = nl * c + i
-        row = rr + odd * (ntp - 1 - 2 * rr)
-        same = (row == y) & (lax.div(y, 2) == c)
-        for n, (src, buf) in enumerate(((w1_hbm, w1), (w2_hbm, w2))):
-            @pl.when(jnp.logical_not(same))
-            def _():
-                rcopy(src.at[i], buf.at[0], ws_sem.at[n, i], wr_sem.at[n, 0], mate).wait_send()
+        for n in range(2):
+            for p in range(PARTS):
+                same, _, direct, _, _ = w_copy(i, n, p)
+
+                @pl.when(jnp.logical_not(same))
+                def _():
+                    direct().wait_send()
 
     def drain(m, _):
         cp_rs(zs, zr, m, fz_s, fz_r).wait_send()
@@ -319,11 +407,17 @@
         rcopy(lbuf.at[2], lbuf.at[2], ls_sem.at[1], lr_sem.at[1], prv).wait_send()
 
     for n in range(2):
-        buf, out = ((w1, g1_hbm), (w2, g2_hbm))[n]
-        for b in range(2):
-            send_g(n, b, True)
-        for i in range(nl):
-            rcopy(buf.at[0], out.at[i], gs_sem.at[n, 0], gr_sem.at[n, i], mate).wait_recv()
+        for p in range(PARTS):
+            for b in range(2):
+                same, _, direct, _, _ = g_copy(n, b, p)
+
+                @pl.when(jnp.logical_not(same))
+                def _():
+                    direct().wait_send()
+
+            for i in range(nl):
+                rcopy(wbuf[n].at[0, parts[p]], gout[n].at[i, parts[p]], gs_sem.at[n, 0, p], gr_sem.at[n, i, p],
+                      mate).wait_recv()
 
 
 def solution(mesh):
@@ -346,13 +440,16 @@
             in_specs=[any_] * 4,
             out_specs=(any_, any_, pl.BlockSpec(memory_space=pltpu.VMEM)),
             scratch_shapes=[
-                vm((2, d, fl), BF), vm((2, fl, d), BF),
+                vm((2, d, fl), BF), vm((2, fl, d), BF), vm((2, fl, d), BF), vm((2, d, fl), BF),
                 vm((2, ntok, hd), BF), vm((2, ntok, hd), BF),
                 vm((2, ntok, fl), BF), vm((2, ntok, fl), BF),
                 vm((ntok, hd), BF), vm((ntok, hd), BF),
                 vm((ntok, hd), BF), vm((ntok, hd), BF), vm((ntok, hd), BF), vm((ntok, hd), BF),
                 vm((2, CHUNK, fl), BF), vm((CHUNK, hd), F32), vm((8, 128), F32), vm((3, 8, 128), F32),
-                dma((3,)), dma((2, nl)), dma((2, 2)), dma((2, 2)), dma((2, nl)),
+                vm((VIA, d // PARTS, fl), BF), vm((VIA, fl // PARTS, d), BF),
+                vm((VIA, d // PARTS, fl), BF), vm((VIA, fl // PARTS, d), BF),
+                dma((3,)), dma((2, nl, PARTS)), dma((2, 2, PARTS)), dma((2, 2, PARTS)), dma((2, nl, PARTS)),
+                dma((2, VIA)), dma((2, VIA)), dma((2, VIA)), dma((2, VIA)),
                 dma((nc,)), dma((nc,)), dma((nc,)), dma((nc,)), dma((nc,)), dma((nc,)),
                 dma((nc,)), dma((nc,)), dma((nc,)), dma((nc,)), dma((nc,)), dma((nc,)),
                 dma((2,)), dma((2,)),

time: 621 us -> 530 us (0.85)
  Pallas kernels: 606 us -> 515 us
    pallas_call x1, Pallas kernels: 606 us -> 515 us  [body(): pl.pallas_call(functools.partial(kernel, ntp, npp, (nm * b) ** (-0.5)), o...]
where the time goes in v2:
time: 530 us
  Pallas kernels  515 us (97%)
  other arithmetic  13.1 us (2%)
    pallas_call x1, Pallas kernels, body(): pl.pallas_call(functools.partial(kernel, ntp, npp, (nm * b) ** (-0.5)), o...  515 us
    broadcast_in_dim x1, other arithmetic, body(): return (g1.astype(F32)[None], g2.astype(F32)[None], loss.reshape(1))  11.8 us

profile of v2, /device:TPU:97, one launch (start us, length us, event | category | flops | bytes accessed | tf_op | source)
XLA Modules:
  0.0 530.2 jit_solution(1704687729575608781)
XLA Ops:
  0.6 514.7 %step.1 = (bf16[2,1024,1024]{2,1,0:T(8,128)(2,1)}, bf16[2,1024,1024]{2,1,0:T(8,128)(2,1)}, f32[8,128]{1,0:T(8,128)}) custom-call(bf16[2048,1024]{1,0:T(8,128)(2,1)} %bitcast.11, bf16[2048,1024]{1,0:T(8,128)(2,1)} %bitcast.12, bf16[2,1024,1024]{2,1,0:T(8,128)(2,1)} %bitcast.13, bf16[2,1024,1024]{2,1,0:T(8,128)(2,1)} %bitcast.14), custom_call_target="tpu_custom_call" | custom-call | tf_op jit(solution)/shard_map/step/pallas_call | solution.py:436
  515.3 1.3 reduce_sum.9
  517.2 11.8 %bitcast_convert_fusion = (f32[1,2,1024,1024]{3,2,1,0:T(8,128)}, f32[1,2,1024,1024]{3,2,1,0:T(8,128)}) fusion(bf16[2,1024,1024]{2,1,0:T(8,128)(2,1)} %get-tuple-element.7, bf16[2,1024,1024]{2,1,0:T(8,128)(2,1)} %get-tuple-element.6), kind=kLoop, calls=%fused_computation | loop fusion | flops 4194304 | bytes 25165824 | tf_op jit(solution)/shard_map/broadcast_in_dim | solution.py:462

commit v3 on v2

--- a/solution.py
+++ b/solution.py
@@ -13,7 +13,7 @@
 MESH = pl.DeviceIdType.MESH
 CHUNK = 128
 PARTS = 4
-VIA = 3
+VIA = 4
 
 
 def gelu_parts(v):
@@ -29,7 +29,7 @@
 
 
 def kernel(ntp, npp, scale, x_hbm, t_hbm, w1_hbm, w2_hbm, g1_hbm, g2_hbm, loss_ref,
-           w1, w2, w1t, w2t, xs, ds, u, g, hs, hb, zs, zr, zsb, zrb, a_buf, zown, lacc, lbuf, rw1, rw2, rg1, rg2,
+           w1, w2, w1t, w2t, part, xs, ds, u, g, hs, hb, zs, zr, zsb, zrb, a_buf, zown, lacc, lbuf, rg1, rg2,
            in_sem, ws_sem, wr_sem, gs_sem, gr_sem, rws, rwr, rgs, rgr, fl_s, fl_r, fa_s, fa_r, fz_s, fz_r,
            bl_s, bl_r, ba_s, ba_r, bz_s, bz_r, ls_sem, lr_sem):
     ntok, hd = hs.shape
@@ -86,7 +86,6 @@
     parts = [pl.ds(p * rp, rp) for p in range(PARTS)]
     wsrc = (w1_hbm, w2_hbm)
     wbuf = (w1, w2)
-    rwb = (rw1, rw2)
     rgb = (rg1, rg2)
     gout = (g1_hbm, g2_hbm)
     cq = lax.div(y, 2)
@@ -101,7 +100,7 @@
         ss, rs = ws_sem.at[n, i, p], wr_sem.at[n, bq, p]
         same = (row == y) & (cq == c)
         direct = functools.partial(rcopy, src, dst, ss, rs, {'tp': row, 'pp': 2 * xc + cq})
-        relay = functools.partial(rcopy, src, rwb[n].at[max(p - kd, 0)], ss, rwr.at[n, max(p - kd, 0)],
+        relay = functools.partial(rcopy, src, g.at[n, parts[max(p - kd, 0)]], ss, rwr.at[n, max(p - kd, 0)],
                                   {'tp': row, 'pp': 2 * (ncol - 1) + cq})
         local = functools.partial(pltpu.make_async_copy, src, dst, rs)
         return same, src_col & (row == far), direct, relay, local
@@ -138,7 +137,7 @@
         for wait in (False, True):
             for n in range(2):
                 for p in reversed(range(kd, PARTS)):
-                    slot = rwb[n].at[p - kd]
+                    slot = g.at[n, parts[p - kd]]
                     fwd_cp = rcopy(slot, wbuf[n].at[far_b, parts[p]], rws.at[n, p - kd], wr_sem.at[n, far_b, p], home)
                     if wait:
                         fwd_cp.wait_send()
@@ -200,15 +199,19 @@
     tn = fl // 2
 
     def fwd(m, _):
+        rw = rows(m)
+        mine = xs[c, rw, :]
+        for q in range(2):
+            part[q] = dot(mine, w1[q, half_c, :])
+
         @pl.when(jnp.logical_not(first))
         def _():
             cp_ag(xs, o, m, fa_s, fa_r).wait_recv()
 
-        rw = rows(m)
         for q in range(2):
             for t in range(fl // tn):
                 s = pl.ds(t * tn, tn)
-                v = (dot(xs[0, rw, :], w1[q, :hd, s]) + dot(xs[1, rw, :], w1[q, hd:, s])).astype(BF)
+                v = (part[q, :, s] + dot(xs[o, rw, :], w1[q, half_o, s])).astype(BF)
                 u[q, rw, s] = v
                 v = v.astype(F32)
                 a_buf[q, :, s] = (0.5 * v * (1.0 + gelu_parts(v))).astype(BF)
@@ -272,12 +275,15 @@
     get_b(0)
 
     def bwd(m, _):
+        rw = rows(m)
+        mine = ds[c, rw, :]
+        for q in range(2):
+            part[q] = dot(mine, w2t[q, half_c, :])
         cp_ag(ds, o, m, ba_s, ba_r).wait_recv()
-        rw = rows(m)
         for q in range(2):
             for t in range(fl // tn):
                 s = pl.ds(t * tn, tn)
-                da = dot(ds[0, rw, :], w2t[q, :hd, s]) + dot(ds[1, rw, :], w2t[q, hd:, s])
+                da = part[q, :, s] + dot(ds[o, rw, :], w2t[q, half_o, s])
                 v = u[q, rw, s].astype(F32)
                 th = gelu_parts(v)
                 gp = 0.5 * (1.0 + th) + 0.5 * v * (1.0 - th * th) * GC * (1.0 + 0.134145 * v * v)
@@ -441,12 +447,12 @@
             out_specs=(any_, any_, pl.BlockSpec(memory_space=pltpu.VMEM)),
             scratch_shapes=[
                 vm((2, d, fl), BF), vm((2, fl, d), BF), vm((2, fl, d), BF), vm((2, d, fl), BF),
+                vm((2, CHUNK, fl), F32),
                 vm((2, ntok, hd), BF), vm((2, ntok, hd), BF),
                 vm((2, ntok, fl), BF), vm((2, ntok, fl), BF),
                 vm((ntok, hd), BF), vm((ntok, hd), BF),
                 vm((ntok, hd), BF), vm((ntok, hd), BF), vm((ntok, hd), BF), vm((ntok, hd), BF),
                 vm((2, CHUNK, fl), BF), vm((CHUNK, hd), F32), vm((8, 128), F32), vm((3, 8, 128), F32),
-                vm((VIA, d // PARTS, fl), BF), vm((VIA, fl // PARTS, d), BF),
                 vm((VIA, d // PARTS, fl), BF), vm((VIA, fl // PARTS, d), BF),
                 dma((3,)), dma((2, nl, PARTS)), dma((2, 2, PARTS)), dma((2, 2, PARTS)), dma((2, nl, PARTS)),
                 dma((2, VIA)), dma((2, VIA)), dma((2, VIA)), dma((2, VIA)),

time: 530 us -> 526 us (level); the launches traced: 530 us -> 519 us
  Pallas kernels: 515 us -> 503 us
    pallas_call x1, Pallas kernels: 515 us -> 503 us  [body(): pl.pallas_call(functools.partial(kernel, ntp, npp, (nm * b) ** (-0.5)), o...]
where the time goes in v3:
time: 526 us; the launch traced here: 519 us
  Pallas kernels  503 us (96%)
  other arithmetic  13.1 us (2%)
    pallas_call x1, Pallas kernels, body(): pl.pallas_call(functools.partial(kernel, ntp, npp, (nm * b) ** (-0.5)), o...  503 us
    broadcast_in_dim x1, other arithmetic, body(): return (g1.astype(F32)[None], g2.astype(F32)[None], loss.reshape(1))  11.8 us

profile of v3, /device:TPU:97, one launch (start us, length us, event | category | flops | bytes accessed | tf_op | source)
XLA Modules:
  0.0 518.6 jit_solution(12080761529266257475)
XLA Ops:
  0.6 503.1 %step.1 = (bf16[2,1024,1024]{2,1,0:T(8,128)(2,1)}, bf16[2,1024,1024]{2,1,0:T(8,128)(2,1)}, f32[8,128]{1,0:T(8,128)}) custom-call(bf16[2048,1024]{1,0:T(8,128)(2,1)} %bitcast.11, bf16[2048,1024]{1,0:T(8,128)(2,1)} %bitcast.12, bf16[2,1024,1024]{2,1,0:T(8,128)(2,1)} %bitcast.13, bf16[2,1024,1024]{2,1,0:T(8,128)(2,1)} %bitcast.14), custom_call_target="tpu_custom_call" | custom-call | tf_op jit(solution)/shard_map/step/pallas_call | solution.py:442
  503.8 1.3 reduce_sum.9
  505.7 11.8 %bitcast_convert_fusion = (f32[1,2,1024,1024]{3,2,1,0:T(8,128)}, f32[1,2,1024,1024]{3,2,1,0:T(8,128)}) fusion(bf16[2,1024,1024]{2,1,0:T(8,128)(2,1)} %get-tuple-element.7, bf16[2,1024,1024]{2,1,0:T(8,128)(2,1)} %get-tuple-element.6), kind=kLoop, calls=%fused_computation | loop fusion | flops 4194304 | bytes 25165824 | tf_op jit(solution)/shard_map/broadcast_in_dim | solution.py:468
